TPU v7x, 32 devices: a whole 2x2x4 slice. The times are simulated.
32 devices in a mesh: gx: 4 (over z), gy: 4 (over x, core), gz: 2 (over y).
Axes of the slice: x: 2, y: 2, z: 4, core: 2. Of those that a mesh axis runs over, the one named last changes fastest.
Arguments:
- right_side: bfloat16 [16, 256, 512], P('gz', 'gx', 'gy'), may hold values from -6 to 6
- phase_mask: int32 [16, 256, 512], P('gz', 'gx', 'gy'), may hold values from 0 to 1, as said below
Outputs:
- pressure: float32 [16, 256, 512], P('gz', 'gx', 'gy')
- scaled_residual: float32 [16, 256, 512], P('gz', 'gx', 'gy')
Inputs may be any that keep to these rules, and one draw needn't show every extreme that they name: `phase_mask`: 0 for a gas cell, 1 for a liquid cell.
All inputs are finite; a program needn't handle non-finite values.
Results may differ from a plain program's by a relative error of at most 0.0004.
Values may be sent and summed in bfloat16 or wider, within the bound.
A program may use at most 64 MiB of HBM per device.

v0:
```python
import jax
import jax.numpy as jnp
from jax import lax
from jax.sharding import PartitionSpec as P

ITERS = 3
density_ratio = 1000.0
mass_shift = 0.05


def padded_2(cells, sides, width):
    for axis, dim in sides:
        count = lax.axis_size(axis)
        head = lax.slice_in_dim(cells, 0, width, axis=dim)
        tail = lax.slice_in_dim(cells, cells.shape[dim] - width, cells.shape[dim], axis=dim)
        cells = jnp.concatenate(
            [
                lax.ppermute(tail, axis, [(i, (i + 1) % count) for i in range(count)]),
                cells,
                lax.ppermute(head, axis, [((i + 1) % count, i) for i in range(count)]),
            ],
            axis=dim,
        )
    return cells


def neighbour(padded, axis, start):
    window = [slice(1, -1), slice(1, -1), slice(1, -1)]
    length = padded.shape[axis] - 2
    window[axis] = slice(start, start + length)
    return padded[tuple(window)]


def centre(padded):
    return padded[1:-1, 1:-1, 1:-1]


def apply_padded(field, padded, weights):
    total = mass_shift * field
    for weight, axis, start in weights:
        total = total + weight * (field - neighbour(padded, axis, start))
    return total


def operate(field, weights):
    padded = padded_2(field, (("gx", 1), ("gy", 2), ("gz", 0)), 1)
    return apply_padded(field, padded, weights)


def products(first, second, third, fourth):
    return lax.psum((jnp.sum(first * second), jnp.sum(third * fourth)), ("gx", "gy", "gz"))


def build_weights(density_padded):
    density = centre(density_padded)
    weights = []
    diagonal = jnp.full(density.shape, mass_shift, jnp.float32)
    for axis in range(3):
        for start in (0, 2):
            weight = 2.0 / (density + neighbour(density_padded, axis, start))
            weights.append((weight, axis, start))
            diagonal = diagonal + weight
    return (weights, diagonal)


def on_device(right_side, phase_mask):
    mask_padded = padded_2(phase_mask, (("gx", 1), ("gy", 2), ("gz", 0)), 1)
    density_padded = 1.0 + (density_ratio - 1.0) * mask_padded.astype(jnp.float32)
    weights, diagonal = build_weights(density_padded)
    source = diagonal * right_side.astype(jnp.float32)
    smoothed = source / diagonal
    first_padded = padded_2(
        smoothed.astype(jnp.bfloat16), (("gx", 1), ("gy", 2), ("gz", 0)), 1
    ).astype(smoothed.dtype)
    applied = apply_padded(smoothed, first_padded, weights)
    pressure = jnp.zeros_like(source)
    residual = source
    direction = smoothed
    direction_image = applied
    scaled_update = smoothed
    twice_update = applied
    energy_old = jnp.float32(1.0)
    step_old = jnp.float32(1.0)
    for iteration in range(ITERS):
        energy, curvature = products(residual, smoothed, applied, smoothed)
        final_turn = iteration + 1 == ITERS
        if not final_turn:
            scaled_applied = applied / diagonal
            applied_twice = operate(scaled_applied, weights)
        if iteration == 0:
            step_size = energy / curvature
            direction = smoothed
            direction_image = applied
            scaled_update = scaled_applied
            twice_update = applied_twice
        else:
            factor = energy / energy_old
            step_size = energy / (curvature - factor * energy / step_old)
            direction = smoothed + factor * direction
            direction_image = applied + factor * direction_image
            if not final_turn:
                scaled_update = scaled_applied + factor * scaled_update
                twice_update = applied_twice + factor * twice_update
        pressure = pressure + step_size * direction
        residual = residual - step_size * direction_image
        if not final_turn:
            smoothed = smoothed - step_size * scaled_update
            applied = applied - step_size * twice_update
        energy_old = energy
        step_old = step_size
    return (pressure, residual / diagonal)


def solution(mesh):
    return jax.shard_map(
        on_device,
        mesh=mesh,
        in_specs=(P("gz", "gx", "gy"), P("gz", "gx", "gy")),
        out_specs=(P("gz", "gx", "gy"), P("gz", "gx", "gy")),
        check_vma=False,
    )
```

profile of v0, /device:TPU:0, one launch (start us, length us, event | category | flops | bytes accessed | tf_op | source)
XLA Modules:
  0.0 218.4 jit_solution(12359695470842941293)
XLA Ops:
  1.4 3.1 %collective-permute-start = (s32[8,1,128]{2,1,0:T(1,128)S(1)}, s32[8,1,128]{2,1,0:T(1,128)S(1)}, u32[]{:S(2)}, u32[]{:S(2)}) collective-permute-start(s32[8,1,128]{2,1,0:T(1,128)S(1)} %get-tuple-element.48), channel_id=1, source_target_pairs={{0,8},{8,16},{16,24},{24,0},{1,9},{9,17},{17,25},{25,1},{2,10},{10... | collective-permute-start | bytes 12296 | tf_op jit(solution)/shard_map/ppermute | solution.py:18
  4.5 2.1 collective-permute-start.1
  9.3 1.7 collective-permute-start.3
  11.1 5.6 %collective-permute-done.2 = s32[8,66,1]{2,1,0:T(8,128)S(1)} collective-permute-done((s32[8,66,1]{2,1,0:T(8,128)S(1)}, s32[8,66,1]{2,1,0:T(8,128)S(1)}, u32[]{:S(2)}, u32[]{:S(2)}) %collective-permute-start.2) | collective-permute-done | bytes 2144 | tf_op jit(solution)/shard_map/ppermute | solution.py:18
  18.0 1.6 collective-permute-start.4
  20.0 2.9 %collective-permute-done.4 = s32[1,66,130]{2,1,0:T(8,128)S(1)} collective-permute-done((s32[1,66,130]{2,1,0:T(8,128)S(1)}, s32[1,66,130]{2,1,0:T(8,128)S(1)}, u32[]{:S(2)}, u32[]{:S(2)}) %collective-permute-start.4) | collective-permute-done | bytes 34352 | tf_op jit(solution)/shard_map/ppermute | solution.py:18
  26.9 2.4 %collective-permute-start.7 = (bf16[8,1,128]{2,1,0:T(2,128)(2,1)S(1)}, bf16[8,1,128]{2,1,0:T(2,128)(2,1)S(1)}, u32[]{:S(2)}, u32[]{:S(2)}) collective-permute-start(bf16[8,1,128]{2,1,0:T(2,128)(2,1)S(1)} %get-tuple-element.53), channel_id=1, source_target_pairs={{8,0},{16,8},{24,16},{0,24},{9,1},{17,9},{25,17},{1,25},{10,2},{18... | collective-permute-start | bytes 6152 | tf_op jit(solution)/shard_map/ppermute | solution.py:20
  31.0 1.7 collective-permute-start.9
  32.7 2.8 %collective-permute-done.8 = bf16[8,66,1]{2,1,0:T(8,128)(2,1)S(1)} collective-permute-done((bf16[8,66,1]{2,1,0:T(8,128)(2,1)S(1)}, bf16[8,66,1]{2,1,0:T(8,128)(2,1)S(1)}, u32[]{:S(2)}, u32[]{:S(2)}) %collective-permute-start.8) | collective-permute-done | bytes 1088 | tf_op jit(solution)/shard_map/ppermute | solution.py:18
  36.4 1.6 collective-permute-start.10
  38.5 2.3 %collective-permute-done.10 = bf16[1,66,130]{2,1,0:T(8,128)(2,1)S(1)} collective-permute-done((bf16[1,66,130]{2,1,0:T(8,128)(2,1)S(1)}, bf16[1,66,130]{2,1,0:T(8,128)(2,1)S(1)}, u32[]{:S(2)}, u32[]{:S(2)}) %collective-permute-start.10) | collective-permute-done | bytes 17192 | tf_op jit(solution)/shard_map/ppermute | solution.py:18
  44.7 2.8 %collective-permute-start.13 = (f32[8,1,128]{2,1,0:T(1,128)S(1)}, f32[8,1,128]{2,1,0:T(1,128)S(1)}, u32[]{:S(2)}, u32[]{:S(2)}) collective-permute-start(f32[8,1,128]{2,1,0:T(1,128)S(1)} %get-tuple-element.47), channel_id=1, source_target_pairs={{8,0},{16,8},{24,16},{0,24},{9,1},{17,9},{25,17},{1,25},{10,2},{18... | collective-permute-start | bytes 12296 | tf_op jit(solution)/shard_map/ppermute | solution.py:20
  49.3 1.7 collective-permute-start.15
  51.0 5.7 %collective-permute-done.14 = f32[8,66,1]{2,1,0:T(8,128)S(1)} collective-permute-done((f32[8,66,1]{2,1,0:T(8,128)S(1)}, f32[8,66,1]{2,1,0:T(8,128)S(1)}, u32[]{:S(2)}, u32[]{:S(2)}) %collective-permute-start.14) | collective-permute-done | bytes 2144 | tf_op jit(solution)/shard_map/ppermute | solution.py:18
  60.4 40.0 %all-reduce.2 = (f32[]{:T(128)}, f32[]{:T(128)}) all-reduce(f32[]{:T(128)} %get-tuple-element.5, f32[]{:T(128)} %get-tuple-element.4), channel_id=1, replica_groups=mesh['gx'=4,'gy'=4,'gz'=2] {'gx','gy','gz'}, use_global_device_ids=true, to_apply=%region_1.0 | all-reduce | flops 2 | bytes 16 | tf_op jit(solution)/shard_map/psum | solution.py:51
  103.2 1.9 collective-permute-start.18
  105.1 2.0 collective-permute-start.19
  109.0 1.7 collective-permute-start.21
  110.7 5.0 %collective-permute-done.20 = f32[8,66,1]{2,1,0:T(8,128)S(1)} collective-permute-done((f32[8,66,1]{2,1,0:T(8,128)S(1)}, f32[8,66,1]{2,1,0:T(8,128)S(1)}, u32[]{:S(2)}, u32[]{:S(2)}) %collective-permute-start.20) | collective-permute-done | bytes 2144 | tf_op jit(solution)/shard_map/ppermute | solution.py:18
  115.7 2.4 %collective-permute-done.21 = f32[8,66,1]{2,1,0:T(8,128)S(1)} collective-permute-done((f32[8,66,1]{2,1,0:T(8,128)S(1)}, f32[8,66,1]{2,1,0:T(8,128)S(1)}, u32[]{:S(2)}, u32[]{:S(2)}) %collective-permute-start.21) | collective-permute-done | bytes 2144 | tf_op jit(solution)/shard_map/ppermute | solution.py:20
  121.6 40.3 %all-reduce.1 = (f32[]{:T(128)}, f32[]{:T(128)}) all-reduce(f32[]{:T(128)} %get-tuple-element.3, f32[]{:T(128)} %get-tuple-element.2), channel_id=1, replica_groups=mesh['gx'=4,'gy'=4,'gz'=2] {'gx','gy','gz'}, use_global_device_ids=true, to_apply=%region_5.0 | all-reduce | flops 2 | bytes 16 | tf_op jit(solution)/shard_map/psum | solution.py:51
  167.2 3.3 %multiply_reduce_fusion = (f32[]{:T(128)}, f32[]{:T(128)}, f32[8,64,128]{2,1,0:T(8,128)S(1)}, f32[8,64,128]{2,1,0:T(8,128)}) fusion(f32[8,64,128]{2,1,0:T(8,128)S(1)} %get-tuple-element.18, f32[8,64,128]{2,1,0:T(8,128)S(1)} %get-tuple-element.19, f32[]{:T(128)S(6)} %div.60, f32[8,64,128]{2,1,0:T(8,128)S(1)} %get-tuple-element.17, f32[]{:T(128)S(6)} %div.58, ...), kind=kLoop, calls=%fused_computation.114 | loop fusion | flops 3997694 | bytes 3882164 | tf_op jit(solution)/shard_map/reduce_sum | solution.py:51
  170.4 42.1 %all-reduce = (f32[]{:T(128)}, f32[]{:T(128)}) all-reduce(f32[]{:T(128)} %get-tuple-element.7, f32[]{:T(128)} %get-tuple-element.6), channel_id=1, replica_groups=mesh['gx'=4,'gy'=4,'gz'=2] {'gx','gy','gz'}, use_global_device_ids=true, to_apply=%region_9.0 | all-reduce | flops 2 | bytes 16 | tf_op jit(solution)/shard_map/psum | solution.py:51
  216.4 2.0 subtract_divide_fusion
  (64 shorter events, 29.0 us)
Async XLA Ops:
  1.4 6.7 %collective-permute-start = (s32[8,1,128]{2,1,0:T(1,128)S(1)}, s32[8,1,128]{2,1,0:T(1,128)S(1)}, u32[]{:S(2)}, u32[]{:S(2)}) collective-permute-start(s32[8,1,128]{2,1,0:T(1,128)S(1)} %get-tuple-element.48), channel_id=1, source_target_pairs={{0,8},{8,16},{16,24},{24,0},{1,9},{9,17},{17,25},{25,1},{2,10},{10... | collective-permute-start | bytes 12296 | tf_op jit(solution)/shard_map/ppermute | solution.py:18
  4.5 3.7 %collective-permute-start.1 = (s32[8,1,128]{2,1,0:T(1,128)S(1)}, s32[8,1,128]{2,1,0:T(1,128)S(1)}, u32[]{:S(2)}, u32[]{:S(2)}) collective-permute-start(s32[8,1,128]{2,1,0:T(1,128)S(1)} %get-tuple-element.49), channel_id=1, source_target_pairs={{8,0},{16,8},{24,16},{0,24},{9,1},{17,9},{25,17},{1,25},{10,2},{18... | collective-permute-start | bytes 12296 | tf_op jit(solution)/shard_map/ppermute | solution.py:20
  9.3 7.4 %collective-permute-start.2 = (s32[8,66,1]{2,1,0:T(8,128)S(1)}, s32[8,66,1]{2,1,0:T(8,128)S(1)}, u32[]{:S(2)}, u32[]{:S(2)}) collective-permute-start(s32[8,66,1]{2,1,0:T(8,128)S(1)} %get-tuple-element.40), channel_id=1, source_target_pairs={{0,2},{2,4},{4,6},{6,0},{1,3},{3,5},{5,7},{7,1},{8,10},{10,12},{12... | collective-permute-start | bytes 6344 | tf_op jit(solution)/shard_map/ppermute | solution.py:18
  9.3 8.5 %collective-permute-start.3 = (s32[8,66,1]{2,1,0:T(8,128)S(1)}, s32[8,66,1]{2,1,0:T(8,128)S(1)}, u32[]{:S(2)}, u32[]{:S(2)}) collective-permute-start(s32[8,66,1]{2,1,0:T(8,128)S(1)} %get-tuple-element.41), channel_id=1, source_target_pairs={{2,0},{4,2},{6,4},{0,6},{3,1},{5,3},{7,5},{1,7},{10,8},{12,10},{14... | collective-permute-start | bytes 6344 | tf_op jit(solution)/shard_map/ppermute | solution.py:20
  18.0 5.0 %collective-permute-start.4 = (s32[1,66,130]{2,1,0:T(8,128)S(1)}, s32[1,66,130]{2,1,0:T(8,128)S(1)}, u32[]{:S(2)}, u32[]{:S(2)}) collective-permute-start(s32[1,66,130]{2,1,0:T(8,128)S(1)} %get-tuple-element.32), channel_id=1, source_target_pairs={{0,1},{1,0},{2,3},{3,2},{4,5},{5,4},{6,7},{7,6},{8,9},{9,8},{10,11... | collective-permute-start | bytes 102968 | tf_op jit(solution)/shard_map/ppermute | solution.py:18
  19.5 4.9 %collective-permute-start.5 = (s32[1,66,130]{2,1,0:T(8,128)S(1)}, s32[1,66,130]{2,1,0:T(8,128)S(1)}, u32[]{:S(2)}, u32[]{:S(2)}) collective-permute-start(s32[1,66,130]{2,1,0:T(8,128)S(1)} %get-tuple-element.33), channel_id=1, source_target_pairs={{1,0},{0,1},{3,2},{2,3},{5,4},{4,5},{7,6},{6,7},{9,8},{8,9},{11,10... | collective-permute-start | bytes 102968 | tf_op jit(solution)/shard_map/ppermute | solution.py:20
  25.3 5.5 %collective-permute-start.6 = (bf16[8,1,128]{2,1,0:T(2,128)(2,1)S(1)}, bf16[8,1,128]{2,1,0:T(2,128)(2,1)S(1)}, u32[]{:S(2)}, u32[]{:S(2)}) collective-permute-start(bf16[8,1,128]{2,1,0:T(2,128)(2,1)S(1)} %get-tuple-element.52), channel_id=1, source_target_pairs={{0,8},{8,16},{16,24},{24,0},{1,9},{9,17},{17,25},{25,1},{2,10},{10... | collective-permute-start | bytes 6152 | tf_op jit(solution)/shard_map/ppermute | solution.py:18
  26.9 3.9 %collective-permute-start.7 = (bf16[8,1,128]{2,1,0:T(2,128)(2,1)S(1)}, bf16[8,1,128]{2,1,0:T(2,128)(2,1)S(1)}, u32[]{:S(2)}, u32[]{:S(2)}) collective-permute-start(bf16[8,1,128]{2,1,0:T(2,128)(2,1)S(1)} %get-tuple-element.53), channel_id=1, source_target_pairs={{8,0},{16,8},{24,16},{0,24},{9,1},{17,9},{25,17},{1,25},{10,2},{18... | collective-permute-start | bytes 6152 | tf_op jit(solution)/shard_map/ppermute | solution.py:20
  30.9 4.6 %collective-permute-start.8 = (bf16[8,66,1]{2,1,0:T(8,128)(2,1)S(1)}, bf16[8,66,1]{2,1,0:T(8,128)(2,1)S(1)}, u32[]{:S(2)}, u32[]{:S(2)}) collective-permute-start(bf16[8,66,1]{2,1,0:T(8,128)(2,1)S(1)} %get-tuple-element.50), channel_id=1, source_target_pairs={{0,2},{2,4},{4,6},{6,0},{1,3},{3,5},{5,7},{7,1},{8,10},{10,12},{12... | collective-permute-start | bytes 3176 | tf_op jit(solution)/shard_map/ppermute | solution.py:18
  31.0 5.3 %collective-permute-start.9 = (bf16[8,66,1]{2,1,0:T(8,128)(2,1)S(1)}, bf16[8,66,1]{2,1,0:T(8,128)(2,1)S(1)}, u32[]{:S(2)}, u32[]{:S(2)}) collective-permute-start(bf16[8,66,1]{2,1,0:T(8,128)(2,1)S(1)} %get-tuple-element.51), channel_id=1, source_target_pairs={{2,0},{4,2},{6,4},{0,6},{3,1},{5,3},{7,5},{1,7},{10,8},{12,10},{14... | collective-permute-start | bytes 3176 | tf_op jit(solution)/shard_map/ppermute | solution.py:20
  36.4 4.4 %collective-permute-start.10 = (bf16[1,66,130]{2,1,0:T(8,128)(2,1)S(1)}, bf16[1,66,130]{2,1,0:T(8,128)(2,1)S(1)}, u32[]{:S(2)}, u32[]{:S(2)}) collective-permute-start(bf16[1,66,130]{2,1,0:T(8,128)(2,1)S(1)} %get-tuple-element.34), channel_id=1, source_target_pairs={{0,1},{1,0},{2,3},{3,2},{4,5},{5,4},{6,7},{7,6},{8,9},{9,8},{10,11... | collective-permute-start | bytes 51488 | tf_op jit(solution)/shard_map/ppermute | solution.py:18
  38.0 4.1 %collective-permute-start.11 = (bf16[1,66,130]{2,1,0:T(8,128)(2,1)S(1)}, bf16[1,66,130]{2,1,0:T(8,128)(2,1)S(1)}, u32[]{:S(2)}, u32[]{:S(2)}) collective-permute-start(bf16[1,66,130]{2,1,0:T(8,128)(2,1)S(1)} %get-tuple-element.35), channel_id=1, source_target_pairs={{1,0},{0,1},{3,2},{2,3},{5,4},{4,5},{7,6},{6,7},{9,8},{8,9},{11,10... | collective-permute-start | bytes 51488 | tf_op jit(solution)/shard_map/ppermute | solution.py:20
  43.5 5.5 %collective-permute-start.12 = (f32[8,1,128]{2,1,0:T(1,128)S(1)}, f32[8,1,128]{2,1,0:T(1,128)S(1)}, u32[]{:S(2)}, u32[]{:S(2)}) collective-permute-start(f32[8,1,128]{2,1,0:T(1,128)S(1)} %get-tuple-element.46), channel_id=1, source_target_pairs={{0,8},{8,16},{16,24},{24,0},{1,9},{9,17},{17,25},{25,1},{2,10},{10... | collective-permute-start | bytes 12296 | tf_op jit(solution)/shard_map/ppermute | solution.py:18
  44.7 4.3 %collective-permute-start.13 = (f32[8,1,128]{2,1,0:T(1,128)S(1)}, f32[8,1,128]{2,1,0:T(1,128)S(1)}, u32[]{:S(2)}, u32[]{:S(2)}) collective-permute-start(f32[8,1,128]{2,1,0:T(1,128)S(1)} %get-tuple-element.47), channel_id=1, source_target_pairs={{8,0},{16,8},{24,16},{0,24},{9,1},{17,9},{25,17},{1,25},{10,2},{18... | collective-permute-start | bytes 12296 | tf_op jit(solution)/shard_map/ppermute | solution.py:20
  49.2 7.5 %collective-permute-start.14 = (f32[8,66,1]{2,1,0:T(8,128)S(1)}, f32[8,66,1]{2,1,0:T(8,128)S(1)}, u32[]{:S(2)}, u32[]{:S(2)}) collective-permute-start(f32[8,66,1]{2,1,0:T(8,128)S(1)} %get-tuple-element.38), channel_id=1, source_target_pairs={{0,2},{2,4},{4,6},{6,0},{1,3},{3,5},{5,7},{7,1},{8,10},{10,12},{12... | collective-permute-start | bytes 6344 | tf_op jit(solution)/shard_map/ppermute | solution.py:18
  49.3 8.3 %collective-permute-start.15 = (f32[8,66,1]{2,1,0:T(8,128)S(1)}, f32[8,66,1]{2,1,0:T(8,128)S(1)}, u32[]{:S(2)}, u32[]{:S(2)}) collective-permute-start(f32[8,66,1]{2,1,0:T(8,128)S(1)} %get-tuple-element.39), channel_id=1, source_target_pairs={{2,0},{4,2},{6,4},{0,6},{3,1},{5,3},{7,5},{1,7},{10,8},{12,10},{14... | collective-permute-start | bytes 6344 | tf_op jit(solution)/shard_map/ppermute | solution.py:20
  58.3 43.4 %collective-permute-start.16 = (f32[1,66,130]{2,1,0:T(8,128)S(1)}, f32[1,66,130]{2,1,0:T(8,128)S(1)}, u32[]{:S(2)}, u32[]{:S(2)}) collective-permute-start(f32[1,66,130]{2,1,0:T(8,128)S(1)} %get-tuple-element.30), channel_id=1, source_target_pairs={{0,1},{1,0},{2,3},{3,2},{4,5},{5,4},{6,7},{7,6},{8,9},{9,8},{10,11... | collective-permute-start | bytes 102968 | tf_op jit(solution)/shard_map/ppermute | solution.py:18
  59.2 42.6 %collective-permute-start.17 = (f32[1,66,130]{2,1,0:T(8,128)S(1)}, f32[1,66,130]{2,1,0:T(8,128)S(1)}, u32[]{:S(2)}, u32[]{:S(2)}) collective-permute-start(f32[1,66,130]{2,1,0:T(8,128)S(1)} %get-tuple-element.31), channel_id=1, source_target_pairs={{1,0},{0,1},{3,2},{2,3},{5,4},{4,5},{7,6},{6,7},{9,8},{8,9},{11,10... | collective-permute-start | bytes 102968 | tf_op jit(solution)/shard_map/ppermute | solution.py:20
  103.2 5.5 %collective-permute-start.18 = (f32[8,1,128]{2,1,0:T(1,128)S(1)}, f32[8,1,128]{2,1,0:T(1,128)S(1)}, u32[]{:S(2)}, u32[]{:S(2)}) collective-permute-start(f32[8,1,128]{2,1,0:T(1,128)S(1)} %get-tuple-element.44), channel_id=1, source_target_pairs={{0,8},{8,16},{16,24},{24,0},{1,9},{9,17},{17,25},{25,1},{2,10},{10... | collective-permute-start | bytes 12296 | tf_op jit(solution)/shard_map/ppermute | solution.py:18
  105.1 3.6 %collective-permute-start.19 = (f32[8,1,128]{2,1,0:T(1,128)S(1)}, f32[8,1,128]{2,1,0:T(1,128)S(1)}, u32[]{:S(2)}, u32[]{:S(2)}) collective-permute-start(f32[8,1,128]{2,1,0:T(1,128)S(1)} %get-tuple-element.45), channel_id=1, source_target_pairs={{8,0},{16,8},{24,16},{0,24},{9,1},{17,9},{25,17},{1,25},{10,2},{18... | collective-permute-start | bytes 12296 | tf_op jit(solution)/shard_map/ppermute | solution.py:20
  108.9 6.8 %collective-permute-start.20 = (f32[8,66,1]{2,1,0:T(8,128)S(1)}, f32[8,66,1]{2,1,0:T(8,128)S(1)}, u32[]{:S(2)}, u32[]{:S(2)}) collective-permute-start(f32[8,66,1]{2,1,0:T(8,128)S(1)} %get-tuple-element.36), channel_id=1, source_target_pairs={{0,2},{2,4},{4,6},{6,0},{1,3},{3,5},{5,7},{7,1},{8,10},{10,12},{12... | collective-permute-start | bytes 6344 | tf_op jit(solution)/shard_map/ppermute | solution.py:18
  109.0 9.1 %collective-permute-start.21 = (f32[8,66,1]{2,1,0:T(8,128)S(1)}, f32[8,66,1]{2,1,0:T(8,128)S(1)}, u32[]{:S(2)}, u32[]{:S(2)}) collective-permute-start(f32[8,66,1]{2,1,0:T(8,128)S(1)} %get-tuple-element.37), channel_id=1, source_target_pairs={{2,0},{4,2},{6,4},{0,6},{3,1},{5,3},{7,5},{1,7},{10,8},{12,10},{14... | collective-permute-start | bytes 6344 | tf_op jit(solution)/shard_map/ppermute | solution.py:20
  118.8 47.7 %collective-permute-start.22 = (f32[1,66,130]{2,1,0:T(8,128)S(1)}, f32[1,66,130]{2,1,0:T(8,128)S(1)}, u32[]{:S(2)}, u32[]{:S(2)}) collective-permute-start(f32[1,66,130]{2,1,0:T(8,128)S(1)} %get-tuple-element.28), channel_id=1, source_target_pairs={{0,1},{1,0},{2,3},{3,2},{4,5},{5,4},{6,7},{7,6},{8,9},{9,8},{10,11... | collective-permute-start | bytes 102968 | tf_op jit(solution)/shard_map/ppermute | solution.py:18
  120.3 46.3 %collective-permute-start.23 = (f32[1,66,130]{2,1,0:T(8,128)S(1)}, f32[1,66,130]{2,1,0:T(8,128)}, u32[]{:S(2)}, u32[]{:S(2)}) collective-permute-start(f32[1,66,130]{2,1,0:T(8,128)S(1)} %get-tuple-element.29), channel_id=1, source_target_pairs={{1,0},{0,1},{3,2},{2,3},{5,4},{4,5},{7,6},{6,7},{9,8},{8,9},{11,10... | collective-permute-start | bytes 102968 | tf_op jit(solution)/shard_map/ppermute | solution.py:20
  (6 other events, 18.5 us)
where the time goes:
time: 219 us; the launch traced here: 218 us
  blocking collectives  122 us (56%)
  waiting for transfers between devices  38.5 us (18%)
  starting transfers between devices  32.4 us (15%)
  other arithmetic  11.3 us (5%)
  between operations  10.7 us (5%)
  local copies, waits for them, and re-layouts  3.12 us (1%)
    psum x3, blocking collectives, products(): lax.psum((jnp.sum(first * second), jnp.sum(third * fourth)), ('gx', 'gy',...  122 us
    ppermute x12, waiting for transfers between devices, padded_2(): lax.ppermute(tail, axis, [(i, (i + 1) % count) for i in range(count)])  30.6 us
    ppermute x12, starting transfers between devices, padded_2(): lax.ppermute(head, axis, [((i + 1) % count, i) for i in range(count)])  19 us
    ppermute x12, starting transfers between devices, padded_2(): lax.ppermute(tail, axis, [(i, (i + 1) % count) for i in range(count)])  13.4 us
    ppermute x12, waiting for transfers between devices, padded_2(): lax.ppermute(head, axis, [((i + 1) % count, i) for i in range(count)])  7.98 us
    reduce_sum x3, other arithmetic, products(): jnp.sum(third * fourth)  5.16 us
  transfers between devices with their start and end apart: 24, of which 17 were waited for; matrix products, arithmetic and copies ran while one was open for 0% of the time, Pallas kernels for 0%

commit v1 on v0

--- a/solution.py
+++ b/solution.py
@@ -6,6 +6,11 @@
 ITERS = 3
 density_ratio = 1000.0
 mass_shift = 0.05
+
+
+def axis_by_axis(array, inner_axis, outer_axis):
+    partial = lax.psum(array, inner_axis)
+    return lax.psum(partial, outer_axis)
 
 
 def padded_2(cells, sides, width):
@@ -48,7 +53,7 @@
 
 
 def products(first, second, third, fourth):
-    return lax.psum((jnp.sum(first * second), jnp.sum(third * fourth)), ("gx", "gy", "gz"))
+    return axis_by_axis((jnp.sum(first * second), jnp.sum(third * fourth)), ("gy", "gz"), "gx")
 
 
 def build_weights(density_padded):

time: 219 us -> 172 us (0.79)
  blocking collectives: 122 us -> 76.2 us
    psum x3 -> x6, blocking collectives: 122 us -> 76.2 us  [the longest x3 41.4 us: axis_by_axis(): partial = lax.psum(array, inner_axis)]
    ppermute x12, starting transfers between devices: 13.4 us -> 10.9 us  [padded_2(): lax.ppermute(tail, axis, [(i, (i + 1) % count) for i in range(count)])]
    ppermute x12, starting transfers between devices: 19 us -> 21.5 us  [padded_2(): lax.ppermute(head, axis, [((i + 1) % count, i) for i in range(count)])]
    ppermute x12, waiting for transfers between devices: 7.98 us -> 5.54 us  [padded_2(): lax.ppermute(head, axis, [((i + 1) % count, i) for i in range(count)])]
  transfers between devices with their start and end apart: 24 -> 24, of which waited for: 17 -> 15; matrix products, arithmetic and copies ran while one was open for 0% -> 0% of each run, Pallas kernels for 0% -> 0%
where the time goes in v1:
time: 172 us
  blocking collectives  76.2 us (44%)
  waiting for transfers between devices  37.6 us (22%)
  starting transfers between devices  32.4 us (19%)
  other arithmetic  11.4 us (7%)
  between operations  11 us (6%)
  local copies, waits for them, and re-layouts  3.24 us (2%)
    psum x3, blocking collectives, axis_by_axis(): partial = lax.psum(array, inner_axis)  41.4 us
    psum x3, blocking collectives, axis_by_axis(): return lax.psum(partial, outer_axis)  34.8 us
    ppermute x12, waiting for transfers between devices, padded_2(): lax.ppermute(tail, axis, [(i, (i + 1) % count) for i in range(count)])  32.1 us
    ppermute x12, starting transfers between devices, padded_2(): lax.ppermute(head, axis, [((i + 1) % count, i) for i in range(count)])  21.5 us
    ppermute x12, starting transfers between devices, padded_2(): lax.ppermute(tail, axis, [(i, (i + 1) % count) for i in range(count)])  10.9 us
    ppermute x12, waiting for transfers between devices, padded_2(): lax.ppermute(head, axis, [((i + 1) % count, i) for i in range(count)])  5.54 us
    reduce_sum x3, other arithmetic, products(): jnp.sum(third * fourth)  5.21 us
  transfers between devices with their start and end apart: 24, of which 15 were waited for; matrix products, arithmetic and copies ran while one was open for 0% of the time, Pallas kernels for 0%

profile of v1, /device:TPU:0, one launch (start us, length us, event | category | flops | bytes accessed | tf_op | source)
XLA Modules:
  0.0 171.8 jit_solution(4114740684292452823)
XLA Ops:
  1.4 3.1 %collective-permute-start = (s32[8,1,128]{2,1,0:T(1,128)S(1)}, s32[8,1,128]{2,1,0:T(1,128)S(1)}, u32[]{:S(2)}, u32[]{:S(2)}) collective-permute-start(s32[8,1,128]{2,1,0:T(1,128)S(1)} %get-tuple-element.54), channel_id=1, source_target_pairs={{0,8},{8,16},{16,24},{24,0},{1,9},{9,17},{17,25},{25,1},{2,10},{10... | collective-permute-start | bytes 12296 | tf_op jit(solution)/shard_map/ppermute | solution.py:23
  4.5 2.1 %collective-permute-start.1 = (s32[8,1,128]{2,1,0:T(1,128)S(1)}, s32[8,1,128]{2,1,0:T(1,128)S(1)}, u32[]{:S(2)}, u32[]{:S(2)}) collective-permute-start(s32[8,1,128]{2,1,0:T(1,128)S(1)} %get-tuple-element.55), channel_id=1, source_target_pairs={{8,0},{16,8},{24,16},{0,24},{9,1},{17,9},{25,17},{1,25},{10,2},{18... | collective-permute-start | bytes 12296 | tf_op jit(solution)/shard_map/ppermute | solution.py:25
  9.3 1.7 %collective-permute-start.3 = (s32[8,66,1]{2,1,0:T(8,128)S(1)}, s32[8,66,1]{2,1,0:T(8,128)S(1)}, u32[]{:S(2)}, u32[]{:S(2)}) collective-permute-start(s32[8,66,1]{2,1,0:T(8,128)S(1)} %get-tuple-element.47), channel_id=1, source_target_pairs={{2,0},{4,2},{6,4},{0,6},{3,1},{5,3},{7,5},{1,7},{10,8},{12,10},{14... | collective-permute-start | bytes 6344 | tf_op jit(solution)/shard_map/ppermute | solution.py:25
  11.1 5.6 %collective-permute-done.2 = s32[8,66,1]{2,1,0:T(8,128)S(1)} collective-permute-done((s32[8,66,1]{2,1,0:T(8,128)S(1)}, s32[8,66,1]{2,1,0:T(8,128)S(1)}, u32[]{:S(2)}, u32[]{:S(2)}) %collective-permute-start.2) | collective-permute-done | bytes 2144 | tf_op jit(solution)/shard_map/ppermute | solution.py:23
  18.0 1.6 collective-permute-start.4
  20.0 2.9 %collective-permute-done.4 = s32[1,66,130]{2,1,0:T(8,128)S(1)} collective-permute-done((s32[1,66,130]{2,1,0:T(8,128)S(1)}, s32[1,66,130]{2,1,0:T(8,128)S(1)}, u32[]{:S(2)}, u32[]{:S(2)}) %collective-permute-start.4) | collective-permute-done | bytes 34352 | tf_op jit(solution)/shard_map/ppermute | solution.py:23
  26.9 2.4 %collective-permute-start.7 = (bf16[8,1,128]{2,1,0:T(2,128)(2,1)S(1)}, bf16[8,1,128]{2,1,0:T(2,128)(2,1)S(1)}, u32[]{:S(2)}, u32[]{:S(2)}) collective-permute-start(bf16[8,1,128]{2,1,0:T(2,128)(2,1)S(1)} %get-tuple-element.59), channel_id=1, source_target_pairs={{8,0},{16,8},{24,16},{0,24},{9,1},{17,9},{25,17},{1,25},{10,2},{18... | collective-permute-start | bytes 6152 | tf_op jit(solution)/shard_map/ppermute | solution.py:25
  31.0 1.7 %collective-permute-start.9 = (bf16[8,66,1]{2,1,0:T(8,128)(2,1)S(1)}, bf16[8,66,1]{2,1,0:T(8,128)(2,1)S(1)}, u32[]{:S(2)}, u32[]{:S(2)}) collective-permute-start(bf16[8,66,1]{2,1,0:T(8,128)(2,1)S(1)} %get-tuple-element.57), channel_id=1, source_target_pairs={{2,0},{4,2},{6,4},{0,6},{3,1},{5,3},{7,5},{1,7},{10,8},{12,10},{14... | collective-permute-start | bytes 3176 | tf_op jit(solution)/shard_map/ppermute | solution.py:25
  32.7 2.8 %collective-permute-done.8 = bf16[8,66,1]{2,1,0:T(8,128)(2,1)S(1)} collective-permute-done((bf16[8,66,1]{2,1,0:T(8,128)(2,1)S(1)}, bf16[8,66,1]{2,1,0:T(8,128)(2,1)S(1)}, u32[]{:S(2)}, u32[]{:S(2)}) %collective-permute-start.8) | collective-permute-done | bytes 1088 | tf_op jit(solution)/shard_map/ppermute | solution.py:23
  38.5 2.3 %collective-permute-done.10 = bf16[1,66,130]{2,1,0:T(8,128)(2,1)S(1)} collective-permute-done((bf16[1,66,130]{2,1,0:T(8,128)(2,1)S(1)}, bf16[1,66,130]{2,1,0:T(8,128)(2,1)S(1)}, u32[]{:S(2)}, u32[]{:S(2)}) %collective-permute-start.10) | collective-permute-done | bytes 17192 | tf_op jit(solution)/shard_map/ppermute | solution.py:23
  44.7 2.8 %collective-permute-start.13 = (f32[8,1,128]{2,1,0:T(1,128)S(1)}, f32[8,1,128]{2,1,0:T(1,128)S(1)}, u32[]{:S(2)}, u32[]{:S(2)}) collective-permute-start(f32[8,1,128]{2,1,0:T(1,128)S(1)} %get-tuple-element.53), channel_id=1, source_target_pairs={{8,0},{16,8},{24,16},{0,24},{9,1},{17,9},{25,17},{1,25},{10,2},{18... | collective-permute-start | bytes 12296 | tf_op jit(solution)/shard_map/ppermute | solution.py:25
  49.3 1.7 %collective-permute-start.15 = (f32[8,66,1]{2,1,0:T(8,128)S(1)}, f32[8,66,1]{2,1,0:T(8,128)S(1)}, u32[]{:S(2)}, u32[]{:S(2)}) collective-permute-start(f32[8,66,1]{2,1,0:T(8,128)S(1)} %get-tuple-element.45), channel_id=1, source_target_pairs={{2,0},{4,2},{6,4},{0,6},{3,1},{5,3},{7,5},{1,7},{10,8},{12,10},{14... | collective-permute-start | bytes 6344 | tf_op jit(solution)/shard_map/ppermute | solution.py:25
  51.0 5.7 %collective-permute-done.14 = f32[8,66,1]{2,1,0:T(8,128)S(1)} collective-permute-done((f32[8,66,1]{2,1,0:T(8,128)S(1)}, f32[8,66,1]{2,1,0:T(8,128)S(1)}, u32[]{:S(2)}, u32[]{:S(2)}) %collective-permute-start.14) | collective-permute-done | bytes 2144 | tf_op jit(solution)/shard_map/ppermute | solution.py:23
  60.4 14.1 %all-reduce.2 = (f32[]{:T(128)}, f32[]{:T(128)}) all-reduce(f32[]{:T(128)} %get-tuple-element.5, f32[]{:T(128)} %get-tuple-element.4), channel_id=1, replica_groups=mesh['gx'=4,'gy'=4,'gz'=2] {'gy','gz'}, use_global_device_ids=true, to_apply=%region_1.0 | all-reduce | flops 2 | bytes 16 | tf_op jit(solution)/shard_map/psum | solution.py:12
  74.5 12.9 %all-reduce.5 = (f32[]{:T(128)}, f32[]{:T(128)}) all-reduce(f32[]{:T(128)} %get-tuple-element.12, f32[]{:T(128)} %get-tuple-element.13), channel_id=1, replica_groups=mesh['gx'=4,'gy'=4,'gz'=2] {'gx'}, use_global_device_ids=true, to_apply=%region_2.0 | all-reduce | flops 2 | bytes 16 | tf_op jit(solution)/shard_map/psum | solution.py:13
  90.2 3.8 %collective-permute-start.19 = (f32[8,1,128]{2,1,0:T(1,128)S(1)}, f32[8,1,128]{2,1,0:T(1,128)S(1)}, u32[]{:S(2)}, u32[]{:S(2)}) collective-permute-start(f32[8,1,128]{2,1,0:T(1,128)S(1)} %get-tuple-element.51), channel_id=1, source_target_pairs={{8,0},{16,8},{24,16},{0,24},{9,1},{17,9},{25,17},{1,25},{10,2},{18... | collective-permute-start | bytes 12296 | tf_op jit(solution)/shard_map/ppermute | solution.py:25
  95.9 1.7 %collective-permute-start.21 = (f32[8,66,1]{2,1,0:T(8,128)S(1)}, f32[8,66,1]{2,1,0:T(8,128)S(1)}, u32[]{:S(2)}, u32[]{:S(2)}) collective-permute-start(f32[8,66,1]{2,1,0:T(8,128)S(1)} %get-tuple-element.43), channel_id=1, source_target_pairs={{2,0},{4,2},{6,4},{0,6},{3,1},{5,3},{7,5},{1,7},{10,8},{12,10},{14... | collective-permute-start | bytes 6344 | tf_op jit(solution)/shard_map/ppermute | solution.py:25
  97.6 6.5 %collective-permute-done.20 = f32[8,66,1]{2,1,0:T(8,128)S(1)} collective-permute-done((f32[8,66,1]{2,1,0:T(8,128)S(1)}, f32[8,66,1]{2,1,0:T(8,128)S(1)}, u32[]{:S(2)}, u32[]{:S(2)}) %collective-permute-start.20) | collective-permute-done | bytes 2144 | tf_op jit(solution)/shard_map/ppermute | solution.py:23
  107.8 14.0 %all-reduce.1 = (f32[]{:T(128)}, f32[]{:T(128)}) all-reduce(f32[]{:T(128)} %get-tuple-element.3, f32[]{:T(128)} %get-tuple-element.2), channel_id=1, replica_groups=mesh['gx'=4,'gy'=4,'gz'=2] {'gy','gz'}, use_global_device_ids=true, to_apply=%region_7.0 | all-reduce | flops 2 | bytes 16 | tf_op jit(solution)/shard_map/psum | solution.py:12
  121.8 12.9 %all-reduce.4 = (f32[]{:T(128)}, f32[]{:T(128)}) all-reduce(f32[]{:T(128)} %get-tuple-element.10, f32[]{:T(128)} %get-tuple-element.11), channel_id=1, replica_groups=mesh['gx'=4,'gy'=4,'gz'=2] {'gx'}, use_global_device_ids=true, to_apply=%region_8.0 | all-reduce | flops 2 | bytes 16 | tf_op jit(solution)/shard_map/psum | solution.py:13
  140.1 3.3 %multiply_reduce_fusion = (f32[]{:T(128)}, f32[]{:T(128)}, f32[8,64,128]{2,1,0:T(8,128)S(1)}, f32[8,64,128]{2,1,0:T(8,128)}) fusion(f32[8,64,128]{2,1,0:T(8,128)S(1)} %get-tuple-element.24, f32[8,64,128]{2,1,0:T(8,128)S(1)} %get-tuple-element.25, f32[]{:T(128)S(6)} %div.60, f32[8,64,128]{2,1,0:T(8,128)S(1)} %get-tuple-element.23, f32[]{:T(128)S(6)} %div.58, ...), kind=kLoop, calls=%fused_computation.114 | loop fusion | flops 3997694 | bytes 3882164 | tf_op jit(solution)/shard_map/reduce_sum | solution.py:56
  143.4 13.3 %all-reduce = (f32[]{:T(128)}, f32[]{:T(128)}) all-reduce(f32[]{:T(128)} %get-tuple-element.7, f32[]{:T(128)} %get-tuple-element.6), channel_id=1, replica_groups=mesh['gx'=4,'gy'=4,'gz'=2] {'gy','gz'}, use_global_device_ids=true, to_apply=%region_13.0 | all-reduce | flops 2 | bytes 16 | tf_op jit(solution)/shard_map/psum | solution.py:12
  156.7 9.1 %all-reduce.3 = (f32[]{:T(128)}, f32[]{:T(128)}) all-reduce(f32[]{:T(128)} %get-tuple-element.8, f32[]{:T(128)} %get-tuple-element.9), channel_id=1, replica_groups=mesh['gx'=4,'gy'=4,'gz'=2] {'gx'}, use_global_device_ids=true, to_apply=%region_14.0 | all-reduce | flops 2 | bytes 16 | tf_op jit(solution)/shard_map/psum | solution.py:13
  169.8 2.0 %subtract_divide_fusion = (f32[8,64,128]{2,1,0:T(8,128)}, f32[8,64,128]{2,1,0:T(8,128)}) fusion(f32[8,64,128]{2,1,0:T(8,128)S(1)} %get-tuple-element.27, f32[8,64,128]{2,1,0:T(8,128)S(1)} %get-tuple-element.20, f32[8,64,128]{2,1,0:T(8,128)S(1)} %get-tuple-element.24, f32[]{:T(128)S(6)} %div.64, f32[]{:T(128)S(6)} %div.66, f32[]{:T(128)S(6)} %div.62, ...), kind=kLoop, calls=%fused_computation.112 | loop fusion | flops 1638400 | bytes 2490388 | tf_op jit(solution)/shard_map/div | solution.py:116
  (67 shorter events, 30.8 us)
Async XLA Ops:
  1.4 6.7 %collective-permute-start = (s32[8,1,128]{2,1,0:T(1,128)S(1)}, s32[8,1,128]{2,1,0:T(1,128)S(1)}, u32[]{:S(2)}, u32[]{:S(2)}) collective-permute-start(s32[8,1,128]{2,1,0:T(1,128)S(1)} %get-tuple-element.54), channel_id=1, source_target_pairs={{0,8},{8,16},{16,24},{24,0},{1,9},{9,17},{17,25},{25,1},{2,10},{10... | collective-permute-start | bytes 12296 | tf_op jit(solution)/shard_map/ppermute | solution.py:23
  4.5 3.7 %collective-permute-start.1 = (s32[8,1,128]{2,1,0:T(1,128)S(1)}, s32[8,1,128]{2,1,0:T(1,128)S(1)}, u32[]{:S(2)}, u32[]{:S(2)}) collective-permute-start(s32[8,1,128]{2,1,0:T(1,128)S(1)} %get-tuple-element.55), channel_id=1, source_target_pairs={{8,0},{16,8},{24,16},{0,24},{9,1},{17,9},{25,17},{1,25},{10,2},{18... | collective-permute-start | bytes 12296 | tf_op jit(solution)/shard_map/ppermute | solution.py:25
  9.3 7.4 %collective-permute-start.2 = (s32[8,66,1]{2,1,0:T(8,128)S(1)}, s32[8,66,1]{2,1,0:T(8,128)S(1)}, u32[]{:S(2)}, u32[]{:S(2)}) collective-permute-start(s32[8,66,1]{2,1,0:T(8,128)S(1)} %get-tuple-element.46), channel_id=1, source_target_pairs={{0,2},{2,4},{4,6},{6,0},{1,3},{3,5},{5,7},{7,1},{8,10},{10,12},{12... | collective-permute-start | bytes 6344 | tf_op jit(solution)/shard_map/ppermute | solution.py:23
  9.3 8.5 %collective-permute-start.3 = (s32[8,66,1]{2,1,0:T(8,128)S(1)}, s32[8,66,1]{2,1,0:T(8,128)S(1)}, u32[]{:S(2)}, u32[]{:S(2)}) collective-permute-start(s32[8,66,1]{2,1,0:T(8,128)S(1)} %get-tuple-element.47), channel_id=1, source_target_pairs={{2,0},{4,2},{6,4},{0,6},{3,1},{5,3},{7,5},{1,7},{10,8},{12,10},{14... | collective-permute-start | bytes 6344 | tf_op jit(solution)/shard_map/ppermute | solution.py:25
  18.0 5.0 %collective-permute-start.4 = (s32[1,66,130]{2,1,0:T(8,128)S(1)}, s32[1,66,130]{2,1,0:T(8,128)S(1)}, u32[]{:S(2)}, u32[]{:S(2)}) collective-permute-start(s32[1,66,130]{2,1,0:T(8,128)S(1)} %get-tuple-element.38), channel_id=1, source_target_pairs={{0,1},{1,0},{2,3},{3,2},{4,5},{5,4},{6,7},{7,6},{8,9},{9,8},{10,11... | collective-permute-start | bytes 102968 | tf_op jit(solution)/shard_map/ppermute | solution.py:23
  19.5 4.9 %collective-permute-start.5 = (s32[1,66,130]{2,1,0:T(8,128)S(1)}, s32[1,66,130]{2,1,0:T(8,128)S(1)}, u32[]{:S(2)}, u32[]{:S(2)}) collective-permute-start(s32[1,66,130]{2,1,0:T(8,128)S(1)} %get-tuple-element.39), channel_id=1, source_target_pairs={{1,0},{0,1},{3,2},{2,3},{5,4},{4,5},{7,6},{6,7},{9,8},{8,9},{11,10... | collective-permute-start | bytes 102968 | tf_op jit(solution)/shard_map/ppermute | solution.py:25
  25.3 5.5 %collective-permute-start.6 = (bf16[8,1,128]{2,1,0:T(2,128)(2,1)S(1)}, bf16[8,1,128]{2,1,0:T(2,128)(2,1)S(1)}, u32[]{:S(2)}, u32[]{:S(2)}) collective-permute-start(bf16[8,1,128]{2,1,0:T(2,128)(2,1)S(1)} %get-tuple-element.58), channel_id=1, source_target_pairs={{0,8},{8,16},{16,24},{24,0},{1,9},{9,17},{17,25},{25,1},{2,10},{10... | collective-permute-start | bytes 6152 | tf_op jit(solution)/shard_map/ppermute | solution.py:23
  26.9 3.9 %collective-permute-start.7 = (bf16[8,1,128]{2,1,0:T(2,128)(2,1)S(1)}, bf16[8,1,128]{2,1,0:T(2,128)(2,1)S(1)}, u32[]{:S(2)}, u32[]{:S(2)}) collective-permute-start(bf16[8,1,128]{2,1,0:T(2,128)(2,1)S(1)} %get-tuple-element.59), channel_id=1, source_target_pairs={{8,0},{16,8},{24,16},{0,24},{9,1},{17,9},{25,17},{1,25},{10,2},{18... | collective-permute-start | bytes 6152 | tf_op jit(solution)/shard_map/ppermute | solution.py:25
  30.9 4.6 %collective-permute-start.8 = (bf16[8,66,1]{2,1,0:T(8,128)(2,1)S(1)}, bf16[8,66,1]{2,1,0:T(8,128)(2,1)S(1)}, u32[]{:S(2)}, u32[]{:S(2)}) collective-permute-start(bf16[8,66,1]{2,1,0:T(8,128)(2,1)S(1)} %get-tuple-element.56), channel_id=1, source_target_pairs={{0,2},{2,4},{4,6},{6,0},{1,3},{3,5},{5,7},{7,1},{8,10},{10,12},{12... | collective-permute-start | bytes 3176 | tf_op jit(solution)/shard_map/ppermute | solution.py:23
  31.0 5.3 %collective-permute-start.9 = (bf16[8,66,1]{2,1,0:T(8,128)(2,1)S(1)}, bf16[8,66,1]{2,1,0:T(8,128)(2,1)S(1)}, u32[]{:S(2)}, u32[]{:S(2)}) collective-permute-start(bf16[8,66,1]{2,1,0:T(8,128)(2,1)S(1)} %get-tuple-element.57), channel_id=1, source_target_pairs={{2,0},{4,2},{6,4},{0,6},{3,1},{5,3},{7,5},{1,7},{10,8},{12,10},{14... | collective-permute-start | bytes 3176 | tf_op jit(solution)/shard_map/ppermute | solution.py:25
  36.4 4.4 %collective-permute-start.10 = (bf16[1,66,130]{2,1,0:T(8,128)(2,1)S(1)}, bf16[1,66,130]{2,1,0:T(8,128)(2,1)S(1)}, u32[]{:S(2)}, u32[]{:S(2)}) collective-permute-start(bf16[1,66,130]{2,1,0:T(8,128)(2,1)S(1)} %get-tuple-element.40), channel_id=1, source_target_pairs={{0,1},{1,0},{2,3},{3,2},{4,5},{5,4},{6,7},{7,6},{8,9},{9,8},{10,11... | collective-permute-start | bytes 51488 | tf_op jit(solution)/shard_map/ppermute | solution.py:23
  38.0 4.1 %collective-permute-start.11 = (bf16[1,66,130]{2,1,0:T(8,128)(2,1)S(1)}, bf16[1,66,130]{2,1,0:T(8,128)(2,1)S(1)}, u32[]{:S(2)}, u32[]{:S(2)}) collective-permute-start(bf16[1,66,130]{2,1,0:T(8,128)(2,1)S(1)} %get-tuple-element.41), channel_id=1, source_target_pairs={{1,0},{0,1},{3,2},{2,3},{5,4},{4,5},{7,6},{6,7},{9,8},{8,9},{11,10... | collective-permute-start | bytes 51488 | tf_op jit(solution)/shard_map/ppermute | solution.py:25
  43.5 5.5 %collective-permute-start.12 = (f32[8,1,128]{2,1,0:T(1,128)S(1)}, f32[8,1,128]{2,1,0:T(1,128)S(1)}, u32[]{:S(2)}, u32[]{:S(2)}) collective-permute-start(f32[8,1,128]{2,1,0:T(1,128)S(1)} %get-tuple-element.52), channel_id=1, source_target_pairs={{0,8},{8,16},{16,24},{24,0},{1,9},{9,17},{17,25},{25,1},{2,10},{10... | collective-permute-start | bytes 12296 | tf_op jit(solution)/shard_map/ppermute | solution.py:23
  44.7 4.3 %collective-permute-start.13 = (f32[8,1,128]{2,1,0:T(1,128)S(1)}, f32[8,1,128]{2,1,0:T(1,128)S(1)}, u32[]{:S(2)}, u32[]{:S(2)}) collective-permute-start(f32[8,1,128]{2,1,0:T(1,128)S(1)} %get-tuple-element.53), channel_id=1, source_target_pairs={{8,0},{16,8},{24,16},{0,24},{9,1},{17,9},{25,17},{1,25},{10,2},{18... | collective-permute-start | bytes 12296 | tf_op jit(solution)/shard_map/ppermute | solution.py:25
  49.2 7.5 %collective-permute-start.14 = (f32[8,66,1]{2,1,0:T(8,128)S(1)}, f32[8,66,1]{2,1,0:T(8,128)S(1)}, u32[]{:S(2)}, u32[]{:S(2)}) collective-permute-start(f32[8,66,1]{2,1,0:T(8,128)S(1)} %get-tuple-element.44), channel_id=1, source_target_pairs={{0,2},{2,4},{4,6},{6,0},{1,3},{3,5},{5,7},{7,1},{8,10},{10,12},{12... | collective-permute-start | bytes 6344 | tf_op jit(solution)/shard_map/ppermute | solution.py:23
  49.3 8.3 %collective-permute-start.15 = (f32[8,66,1]{2,1,0:T(8,128)S(1)}, f32[8,66,1]{2,1,0:T(8,128)S(1)}, u32[]{:S(2)}, u32[]{:S(2)}) collective-permute-start(f32[8,66,1]{2,1,0:T(8,128)S(1)} %get-tuple-element.45), channel_id=1, source_target_pairs={{2,0},{4,2},{6,4},{0,6},{3,1},{5,3},{7,5},{1,7},{10,8},{12,10},{14... | collective-permute-start | bytes 6344 | tf_op jit(solution)/shard_map/ppermute | solution.py:25
  58.3 30.3 %collective-permute-start.16 = (f32[1,66,130]{2,1,0:T(8,128)S(1)}, f32[1,66,130]{2,1,0:T(8,128)S(1)}, u32[]{:S(2)}, u32[]{:S(2)}) collective-permute-start(f32[1,66,130]{2,1,0:T(8,128)S(1)} %get-tuple-element.36), channel_id=1, source_target_pairs={{0,1},{1,0},{2,3},{3,2},{4,5},{5,4},{6,7},{7,6},{8,9},{9,8},{10,11... | collective-permute-start | bytes 102968 | tf_op jit(solution)/shard_map/ppermute | solution.py:23
  59.2 29.5 %collective-permute-start.17 = (f32[1,66,130]{2,1,0:T(8,128)S(1)}, f32[1,66,130]{2,1,0:T(8,128)S(1)}, u32[]{:S(2)}, u32[]{:S(2)}) collective-permute-start(f32[1,66,130]{2,1,0:T(8,128)S(1)} %get-tuple-element.37), channel_id=1, source_target_pairs={{1,0},{0,1},{3,2},{2,3},{5,4},{4,5},{7,6},{6,7},{9,8},{8,9},{11,10... | collective-permute-start | bytes 102968 | tf_op jit(solution)/shard_map/ppermute | solution.py:25
  90.1 5.5 %collective-permute-start.18 = (f32[8,1,128]{2,1,0:T(1,128)S(1)}, f32[8,1,128]{2,1,0:T(1,128)S(1)}, u32[]{:S(2)}, u32[]{:S(2)}) collective-permute-start(f32[8,1,128]{2,1,0:T(1,128)S(1)} %get-tuple-element.50), channel_id=1, source_target_pairs={{0,8},{8,16},{16,24},{24,0},{1,9},{9,17},{17,25},{25,1},{2,10},{10... | collective-permute-start | bytes 12296 | tf_op jit(solution)/shard_map/ppermute | solution.py:23
  90.2 5.4 %collective-permute-start.19 = (f32[8,1,128]{2,1,0:T(1,128)S(1)}, f32[8,1,128]{2,1,0:T(1,128)S(1)}, u32[]{:S(2)}, u32[]{:S(2)}) collective-permute-start(f32[8,1,128]{2,1,0:T(1,128)S(1)} %get-tuple-element.51), channel_id=1, source_target_pairs={{8,0},{16,8},{24,16},{0,24},{9,1},{17,9},{25,17},{1,25},{10,2},{18... | collective-permute-start | bytes 12296 | tf_op jit(solution)/shard_map/ppermute | solution.py:25
  95.8 8.3 %collective-permute-start.20 = (f32[8,66,1]{2,1,0:T(8,128)S(1)}, f32[8,66,1]{2,1,0:T(8,128)S(1)}, u32[]{:S(2)}, u32[]{:S(2)}) collective-permute-start(f32[8,66,1]{2,1,0:T(8,128)S(1)} %get-tuple-element.42), channel_id=1, source_target_pairs={{0,2},{2,4},{4,6},{6,0},{1,3},{3,5},{5,7},{7,1},{8,10},{10,12},{12... | collective-permute-start | bytes 6344 | tf_op jit(solution)/shard_map/ppermute | solution.py:23
  95.9 8.2 %collective-permute-start.21 = (f32[8,66,1]{2,1,0:T(8,128)S(1)}, f32[8,66,1]{2,1,0:T(8,128)S(1)}, u32[]{:S(2)}, u32[]{:S(2)}) collective-permute-start(f32[8,66,1]{2,1,0:T(8,128)S(1)} %get-tuple-element.43), channel_id=1, source_target_pairs={{2,0},{4,2},{6,4},{0,6},{3,1},{5,3},{7,5},{1,7},{10,8},{12,10},{14... | collective-permute-start | bytes 6344 | tf_op jit(solution)/shard_map/ppermute | solution.py:25
  104.9 34.5 %collective-permute-start.22 = (f32[1,66,130]{2,1,0:T(8,128)S(1)}, f32[1,66,130]{2,1,0:T(8,128)S(1)}, u32[]{:S(2)}, u32[]{:S(2)}) collective-permute-start(f32[1,66,130]{2,1,0:T(8,128)S(1)} %get-tuple-element.34), channel_id=1, source_target_pairs={{0,1},{1,0},{2,3},{3,2},{4,5},{5,4},{6,7},{7,6},{8,9},{9,8},{10,11... | collective-permute-start | bytes 102968 | tf_op jit(solution)/shard_map/ppermute | solution.py:23
  105.7 33.8 %collective-permute-start.23 = (f32[1,66,130]{2,1,0:T(8,128)S(1)}, f32[1,66,130]{2,1,0:T(8,128)}, u32[]{:S(2)}, u32[]{:S(2)}) collective-permute-start(f32[1,66,130]{2,1,0:T(8,128)S(1)} %get-tuple-element.35), channel_id=1, source_target_pairs={{1,0},{0,1},{3,2},{2,3},{5,4},{4,5},{7,6},{6,7},{9,8},{8,9},{11,10... | collective-permute-start | bytes 102968 | tf_op jit(solution)/shard_map/ppermute | solution.py:25
  (6 other events, 16.8 us)
